TPU v7x, 32 devices: a whole 2x2x4 slice. The times are simulated.
32 devices in a mesh: dp: 8 (over z, core), feat: 4 (over y, x).
Axes of the slice: x: 2, y: 2, z: 4, core: 2. Of those that a mesh axis runs over, the one named last changes fastest.
Arguments:
- points: bfloat16 [2048, 256], P('dp'), may hold values from -6 to 6
- freqs: bfloat16 [256, 8192], P(None, 'feat'), may hold values from -0.375 to 0.375
- phase: float32 [8192], P('feat'), may hold values from -3.140625 to 3.140625
- ridge: float32 [8192], P('feat'), may hold values from 0.05 to 0.5
- targets: bfloat16 [8, 2048], P(None, 'dp'), may hold values from -6 to 6
Outputs:
- gram: float32 [8192, 8192], P('feat', 'dp')
- projected: float32 [8, 8192], P(None, 'feat')
- factors: float32 [8192, 1024], P('feat')
All inputs are finite; a program needn't handle non-finite values.
Results may differ from a plain program's by a relative error of at most 0.003.
Values may be sent and summed in bfloat16 or wider, within the bound.
A program may use at most 128 MiB of HBM per device.

v0:
```python
import functools
import math

import jax
import jax.numpy as jnp
from jax import lax
from jax.experimental import pallas as pl
from jax.experimental.pallas import tpu as pltpu
from jax.sharding import PartitionSpec as P

FB = 1024
TILE = 128
MICRO = 16
WIDE = 256
MIB = 1024 * 1024
COS_TURNS = (
    0.9999991998413438,
    -19.738978175861334,
    64.92858783993428,
    -85.27084362691367,
    58.786940763031694,
    -21.065429407523915,
)


def features(rows, freq_cols, phase_turns, scale):
    angle = jnp.dot(rows, freq_cols, preferred_element_type=jnp.float32)
    return wave(angle * (0.5 / math.pi) + phase_turns, scale)


def wave(turns, scale):
    part = turns - jnp.round(turns)
    square = part * part
    poly = square * (scale * COS_TURNS[-1]) + scale * COS_TURNS[-2]
    for coeff in COS_TURNS[-3::-1]:
        poly = poly * square + scale * coeff
    return poly.astype(jnp.bfloat16)


def cross(left, right):
    return lax.dot_general(
        left, right, (((0,), (0,)), ((), ())), preferred_element_type=jnp.float32
    )


def with_ridge(tile, ridge, row_start, col_start):
    rows_here = row_start + lax.broadcasted_iota(jnp.int32, tile.shape, 0)
    cols_here = col_start + lax.broadcasted_iota(jnp.int32, tile.shape, 1)
    return tile + jnp.where(rows_here == cols_here, ridge, 0.0)


def halves(value):
    high = value.astype(jnp.bfloat16)
    return high, (value - high.astype(jnp.float32)).astype(jnp.bfloat16)


def left_parts(value, axis):
    high, low = halves(value)
    return jnp.concatenate([high, high, low], axis=axis)


def right_parts(value):
    high, low = halves(value)
    return jnp.concatenate([high, low, high], axis=0)


def panel_rows(rows_lead, rows_tail, start):
    shape = rows_lead.shape
    row_ids = lax.broadcasted_iota(jnp.int32, shape, 0)
    cols = [
        jnp.broadcast_to(rows_lead[:, start + i : start + i + 1], shape) for i in range(MICRO)
    ]
    for i in range(MICRO):
        inv = lax.rsqrt(cols[i][i : i + 1, :])
        mult = cols[i] * inv
        for m in range(i + 1, MICRO):
            cols[m] = cols[m] - mult * mult[m : m + 1, :]
        below = jnp.where(row_ids > i, mult, 0.0)
        here = row_ids == i
        lead = rows_lead[i : i + 1, :] * inv
        tail = rows_tail[i : i + 1, :] * inv
        rows_lead = jnp.where(here, lead, rows_lead - below * lead)
        rows_tail = jnp.where(here, tail, rows_tail - below * tail)
    return rows_lead, rows_tail


def factor_steps(work, panel, out, emit, *, count, size):
    tiles = size // TILE
    row_ids = lax.broadcasted_iota(jnp.int32, (TILE, TILE), 0)
    col_ids = lax.broadcasted_iota(jnp.int32, (TILE, TILE), 1)

    def step(k, carry):
        at = pl.multiple_of(k * TILE, TILE)
        for blk in range(count):
            panel[blk, :, :TILE] = work[blk, pl.ds(at, TILE), pl.ds(at, TILE)]
            panel[blk, :, TILE:] = jnp.where(row_ids == col_ids, 1.0, 0.0)
        for start in range(0, TILE, MICRO):
            end = start + MICRO
            for blk in range(count):
                lead, tail = panel_rows(
                    panel[blk, start:end, :TILE], panel[blk, start:end, TILE:], start
                )
                panel[blk, start:end, :TILE] = lead
                panel[blk, start:end, TILE:] = tail
                if end < TILE:
                    left = left_parts(lead, 0)
                    right = right_parts(jnp.concatenate([lead, tail], axis=1))
                    panel[blk, end:, :] = panel[blk, end:, :] - cross(left, right)[end:, :]
        for blk in range(count):
            lower = jnp.where(row_ids >= col_ids, panel[blk, :, :TILE].T, 0.0)
            out[blk, pl.ds(at, TILE), pl.ds(at, TILE)] = lower
        for c in range(tiles - 1):

            @pl.when(k == c)
            def _():
                lo, mid = c * TILE, (c + 1) * TILE
                for blk in range(count):
                    upper = jnp.dot(
                        left_parts(panel[blk, :, TILE:], 1),
                        right_parts(work[blk, lo:mid, mid:]),
                        preferred_element_type=jnp.float32,
                    )
                    lower = upper.T
                    out[blk, mid:, lo:mid] = lower
                    out[blk, lo:mid, mid:] = jnp.zeros_like(upper)
                    left = left_parts(lower, 1)
                    right = right_parts(upper)
                    rest = size - mid
                    for first in range(0, rest, 2 * TILE):
                        last = min(first + 2 * TILE, rest)
                        update = jnp.dot(
                            left[first:last], right[:, first:], preferred_element_type=jnp.float32
                        )
                        r = mid + first
                        work[blk, r : mid + last, r:] = work[blk, r : mid + last, r:] - update

        emit(k)
        return carry

    lax.fori_loop(0, tiles, step, 0)


def across(left, right):
    return lax.dot_general(
        left, right, (((1,), (1,)), ((), ())), preferred_element_type=jnp.float32
    )


def spread_body(points, targets, phase, freqs, phi, points_out, freqs_out, turns_out, projected,
                pbuf, tbuf, fbuf, fown, cbuf, flipped, turns, in_sem,
                psend, precv, tsend, trecv, fsend, frecv, csend, crecv, pass_sem,
                *, data_count, feat_count, scale):
    me = lax.axis_index("dp")
    here = lax.axis_index("feat")
    chips = data_count // 2
    chip, core = me // 2, me % 2
    rows = points.shape[0]
    depth, width = freqs.shape
    tile_width = freqs_out.shape[1]
    partner = chip * 2 + (1 - core)
    holder = me * tile_width // width
    offset = pl.multiple_of(me * tile_width % width, tile_width)
    pieces = cbuf.shape[0]
    piece = tile_width // pieces
    side_x = (here % 2 + holder % 2) % 2
    side_y = (here // 2 + holder // 2) % 2
    opposite = 3 - holder

    loads = [
        pltpu.make_async_copy(points, pbuf.at[me], in_sem.at[0]),
        pltpu.make_async_copy(targets, tbuf.at[me], in_sem.at[1]),
        pltpu.make_async_copy(phase, fbuf.at[here], in_sem.at[2]),
        pltpu.make_async_copy(freqs, fown, in_sem.at[3]),
    ]
    for copy in loads:
        copy.start()

    def remote(source, target, send, recv, dp, feat):
        return pltpu.make_async_remote_copy(
            src_ref=source, dst_ref=target, send_sem=send, recv_sem=recv,
            device_id={"dp": dp, "feat": feat}, device_id_type=pl.DeviceIdType.MESH)

    barrier = pltpu.get_barrier_semaphore()
    for step in range(1, data_count):
        pl.semaphore_signal(
            barrier, inc=1, device_id={"dp": lax.rem(me + step, data_count), "feat": here},
            device_id_type=pl.DeviceIdType.MESH)
    for step in range(1, feat_count):
        pl.semaphore_signal(
            barrier, inc=1, device_id={"dp": me, "feat": lax.rem(here + step, feat_count)},
            device_id_type=pl.DeviceIdType.MESH)
    pl.semaphore_wait(barrier, data_count + feat_count - 2)

    def peer(step):
        return lax.rem(chip + step, chips) * 2 + core

    def points_copy(slot, sem, dp):
        return remote(pbuf.at[slot], pbuf.at[slot], sem, precv.at[slot], dp, here)

    def targets_copy(slot, step):
        dp = lax.rem(me + step, data_count)
        return remote(tbuf.at[slot], tbuf.at[slot], tsend.at[step], trecv.at[slot], dp, here)

    def phase_copy(slot, step):
        feat = lax.rem(here + step, feat_count)
        return remote(fbuf.at[slot], fbuf.at[slot], fsend.at[step], frecv.at[slot], me, feat)

    def freqs_copy(q, way, feat):
        source = fown.at[:, pl.ds(offset + q * piece, piece)]
        return remote(source, cbuf.at[q], csend.at[way * pieces + q], crecv.at[q], me, feat)

    def freqs_pass(q, t):
        return remote(cbuf.at[q], cbuf.at[q], csend.at[t], crecv.at[q], me, opposite)

    order = [(t + 1) // 2 if t % 2 else chips - t // 2 for t in range(1, chips)]
    loads[0].wait()
    points_copy(me, psend.at[0], partner).start()
    for step in order:
        points_copy(me, psend.at[step], peer(step)).start()
    loads[1].wait()
    for step in range(1, data_count):
        targets_copy(me, step).start()
    loads[2].wait()
    for step in range(1, feat_count):
        phase_copy(here, step).start()
    loads[3].wait()
    near_x = (1 - holder % 2) + holder // 2 * 2
    near_y = holder % 2 + (1 - holder // 2) * 2
    sends = [(q, 0, near_x) for q in range(pieces)]
    sends += [((q + pieces // 2) % pieces, 1, near_y) for q in range(pieces)]
    half = pieces // 2

    @pl.when(here == holder)
    def _():
        for q, way, feat in sends:
            freqs_copy(q, way, feat).start()

    flipped[...] = fown[...].T
    for first in range(0, width, TILE):
        row = fbuf[here, :, first : first + TILE] * (0.5 / math.pi)
        turns[first : first + TILE, :] = jnp.broadcast_to(row, (TILE, TILE)).T
    projected[...] = jnp.zeros_like(projected)
    step_width = min(width, 1024)

    def compute(slot):
        at = pl.multiple_of(slot * rows, rows)
        block = pbuf[slot]
        points_out[pl.ds(at, rows), :] = block

        def part(j, carry):
            feats = pl.ds(pl.multiple_of(j * step_width, step_width), step_width)
            angle = across(flipped[feats, :], block) * (0.5 / math.pi)
            shift = turns[feats, :]
            value = wave(angle + jnp.concatenate([shift] * (rows // TILE), axis=1), scale)
            phi[feats, pl.ds(at, rows)] = value
            projected[:, feats] = projected[:, feats] + across(tbuf[slot], value)
            return carry

        lax.fori_loop(0, width // step_width, part, 0)

    def targets_wait(slot):
        remote(tbuf.at[slot], tbuf.at[slot], tsend.at[1], trecv.at[slot], partner, here).wait_recv()

    compute(me)
    points_copy(partner, psend.at[0], partner).wait_recv()
    targets_wait(partner)
    compute(partner)

    def arrive(t, carry):
        odd = t % 2
        step = odd * ((t + 1) // 2) + (1 - odd) * (chips - t // 2)
        source = lax.rem(chip + chips - step, chips)
        same = source * 2 + core
        other = source * 2 + (1 - core)
        points_copy(same, psend.at[0], partner).wait_recv()
        points_copy(same, pass_sem.at[t], partner).start()
        targets_wait(same)
        compute(same)
        points_copy(other, psend.at[0], partner).wait_recv()
        targets_wait(other)
        compute(other)

        @pl.when((side_x + side_y == 1) & (t >= chips - half))
        def _():
            q = side_y * half + t - (chips - half)
            freqs_pass(q, 0).wait_recv()
            freqs_pass(q, t - (chips - half)).start()

        return carry

    lax.fori_loop(1, chips, arrive, 0)

    for step in range(1, feat_count):
        slot = lax.rem(here + step, feat_count)
        phase_copy(slot, step).wait_recv()
    turns_out[...] = fbuf[...] * (0.5 / math.pi)

    @pl.when(here == holder)
    def _():
        freqs_out[...] = fown[:, pl.ds(offset, tile_width)]
        for q, way, feat in sends:
            freqs_copy(q, way, feat).wait_send()

    @pl.when(side_x + side_y == 1)
    def _():
        for t in range(half):
            freqs_pass((1 - side_y) * half + t, 0).wait_recv()
            freqs_pass(side_y * half + t, t).wait_send()

    @pl.when(side_x + side_y == 2)
    def _():
        for q in range(pieces):
            freqs_pass(q, 0).wait_recv()

    @pl.when(here != holder)
    def _():
        for q in range(pieces):
            freqs_out[:, q * piece : (q + 1) * piece] = cbuf[q]

    points_copy(me, psend.at[0], partner).wait_send()
    for step in order:
        points_copy(me, psend.at[step], peer(step)).wait_send()
    for step in range(1, data_count):
        targets_copy(me, step).wait_send()
    for step in range(1, feat_count):
        phase_copy(here, step).wait_send()
    for t in range(1, chips):
        points_copy(me, pass_sem.at[t], partner).wait_send()


def spread(points, targets, phase, freqs, tile_width, scale):
    data_count, feat_count = lax.axis_size("dp"), lax.axis_size("feat")
    rows, depth = points.shape
    width = freqs.shape[1]
    outs = targets.shape[0]
    vmem = pl.BlockSpec(memory_space=pltpu.VMEM)
    hbm = pl.BlockSpec(memory_space=pltpu.HBM)
    dma = pltpu.SemaphoreType.DMA
    pieces = 4
    return pl.pallas_call(
        functools.partial(spread_body, data_count=data_count, feat_count=feat_count, scale=scale),
        out_shape=(
            jax.ShapeDtypeStruct((width, rows * data_count), jnp.bfloat16),
            jax.ShapeDtypeStruct((rows * data_count, depth), jnp.bfloat16),
            jax.ShapeDtypeStruct((depth, tile_width), jnp.bfloat16),
            jax.ShapeDtypeStruct((feat_count, 1, width), jnp.float32),
            jax.ShapeDtypeStruct((outs, width), jnp.float32),
        ),
        in_specs=[hbm] * 4,
        out_specs=[vmem] * 5,
        scratch_shapes=[
            pltpu.VMEM((data_count, rows, depth), jnp.bfloat16),
            pltpu.VMEM((data_count, outs, rows), jnp.bfloat16),
            pltpu.VMEM((feat_count, 1, width), jnp.float32),
            pltpu.VMEM((depth, width), jnp.bfloat16),
            pltpu.VMEM((pieces, depth, tile_width // pieces), jnp.bfloat16),
            pltpu.VMEM((width, depth), jnp.bfloat16),
            pltpu.VMEM((width, TILE), jnp.float32),
            dma((4,)),
            dma((data_count // 2,)),
            dma((data_count,)),
            dma((data_count,)),
            dma((data_count,)),
            dma((feat_count,)),
            dma((feat_count,)),
            dma((2 * pieces,)),
            dma((pieces,)),
            dma((data_count // 2,)),
        ],
        compiler_params=pltpu.CompilerParams(
            collective_id=0, has_side_effects=True, vmem_limit_bytes=24 * MIB
        ),
        cost_estimate=pl.CostEstimate(
            flops=2 * rows * data_count * depth * width,
            bytes_accessed=2 * rows * data_count * width,
            transcendentals=0,
        ),
        name="spread",
    )(points, targets, phase[None, :], freqs)


def factor_body(phi, sums, ridge, out, projected, work, block_out, panel, out_sem,
                *, count, size):
    projected[...] = sums[...]
    for blk in range(count):
        base = blk * size
        for c in range(0, size, WIDE):
            mid = c + WIDE
            tile = across(phi[base : base + mid, :], phi[base + c : base + mid, :])
            work[blk, :mid, c:mid] = with_ridge(tile, ridge[:, base + c : base + mid], 0, c)

    def rows_out(blk, k):
        at = pl.ds(pl.multiple_of(k * TILE, TILE), TILE)
        return pltpu.make_async_copy(block_out.at[blk, at], out.at[blk, at], out_sem.at[blk])

    def emit(k):
        for blk in range(count):
            rows_out(blk, k).start()

    factor_steps(work, panel, block_out, emit, count=count, size=size)
    for blk in range(count):
        pltpu.make_async_copy(block_out.at[blk], out.at[blk], out_sem.at[blk]).wait()


def factor(phi, sums, ridge, size):
    width, rows = phi.shape
    count = width // size
    outs = sums.shape[0]
    vmem = pl.BlockSpec(memory_space=pltpu.VMEM)
    hbm = pl.BlockSpec(memory_space=pltpu.HBM)
    return pl.pallas_call(
        functools.partial(factor_body, count=count, size=size),
        out_shape=(
            jax.ShapeDtypeStruct((count, size, size), jnp.float32),
            jax.ShapeDtypeStruct((outs, width), jnp.float32),
        ),
        in_specs=[vmem] * 3,
        out_specs=(hbm, vmem),
        scratch_shapes=[
            pltpu.VMEM((count, size, size), jnp.float32),
            pltpu.VMEM((count, size, size), jnp.float32),
            pltpu.VMEM((count, TILE, 2 * TILE), jnp.float32),
            pltpu.SemaphoreType.DMA((count,)),
        ],
        compiler_params=pltpu.CompilerParams(vmem_limit_bytes=32 * MIB),
        cost_estimate=pl.CostEstimate(
            flops=30 * rows * width * size, bytes_accessed=8 * rows * width, transcendentals=0
        ),
        name="lower_factors",
    )(phi, sums, ridge)


def tile_body(phi, points, freqs, phase, ridge, start, out, cols_phi, ring, out_sem, *, scale):
    width, rows = phi.shape
    columns = freqs.shape[1]
    slots, tall, _ = ring.shape
    down, wide = width // tall, columns // WIDE
    chunk = rows // down

    def make(j, r):
        cols = pl.ds(pl.multiple_of(j * WIDE, WIDE), WIDE)
        at = pl.ds(pl.multiple_of(r * chunk, chunk), chunk)
        cols_phi[lax.rem(j, 2), at, :] = features(
            points[at, :], freqs[:, cols], phase[:, cols], scale
        )

    def store(j, r, slot):
        return pltpu.make_async_copy(
            ring.at[slot],
            out.at[pl.ds(pl.multiple_of(r * tall, tall), tall),
                   pl.ds(pl.multiple_of(j * WIDE, WIDE), WIDE)],
            out_sem.at[slot])

    def first(r, carry):
        make(0, r)
        return carry

    lax.fori_loop(0, down, first, 0)

    def one(it, carry):
        j, r = it // down, lax.rem(it, down)
        slot = lax.rem(it, slots)

        @pl.when(it >= slots)
        def _():
            store(j, r, slot).wait()

        cols = pl.ds(pl.multiple_of(j * WIDE, WIDE), WIDE)
        at = pl.ds(pl.multiple_of(r * tall, tall), tall)
        tile = jnp.dot(phi[at, :], cols_phi[lax.rem(j, 2)], preferred_element_type=jnp.float32)
        ring[slot] = with_ridge(tile, ridge[:, cols], r * tall, j * WIDE + start[0])
        make(lax.rem(j + 1, wide), r)
        store(j, r, slot).start()
        return carry

    total = down * wide
    lax.fori_loop(0, total, one, 0)
    for it in range(total - slots, total):
        store(it // down, it % down, it % slots).wait()


def gram_tile(phi, points, freqs, phase, ridge, start, scale):
    width, rows = phi.shape
    columns = freqs.shape[1]
    vmem = pl.BlockSpec(memory_space=pltpu.VMEM)
    slots = 3
    return pl.pallas_call(
        functools.partial(tile_body, scale=scale),
        out_shape=jax.ShapeDtypeStruct((width, columns), jnp.float32),
        in_specs=[vmem, vmem, vmem, vmem, vmem, pl.BlockSpec(memory_space=pltpu.SMEM)],
        out_specs=pl.BlockSpec(memory_space=pltpu.HBM),
        scratch_shapes=[
            pltpu.VMEM((2, rows, WIDE), jnp.bfloat16),
            pltpu.VMEM((slots, 2 * WIDE, WIDE), jnp.float32),
            pltpu.SemaphoreType.DMA((slots,)),
        ],
        compiler_params=pltpu.CompilerParams(vmem_limit_bytes=24 * MIB),
        cost_estimate=pl.CostEstimate(
            flops=2 * rows * width * columns, bytes_accessed=4 * width * columns, transcendentals=0
        ),
        name="gram_tile",
    )(phi, points, freqs, phase, ridge, start)


def near_shards(points, freqs, phase, ridge, targets):
    data_count, feat_count = lax.axis_size("dp"), lax.axis_size("feat")
    data_index, feat_index = lax.axis_index("dp"), lax.axis_index("feat")
    local_width = freqs.shape[1]
    tile_width = local_width * feat_count // data_count
    scale = math.sqrt(2.0 / (points.shape[0] * data_count))
    phi, points_all, col_freqs, turns, sums = spread(
        points, targets, phase, freqs, tile_width, scale
    )
    factors, projected = factor(phi, sums, ridge[None, :], FB)
    col_start = data_index * tile_width
    start = col_start - feat_index * local_width
    col_turns = lax.dynamic_slice_in_dim(turns.reshape(1, -1), col_start, tile_width, 1)
    col_ridge = lax.dynamic_slice_in_dim(ridge[None, :], start, tile_width, 1)
    gram = gram_tile(phi, points_all, col_freqs, col_turns, col_ridge, start[None], scale)
    return gram, projected, factors.reshape(local_width, FB)


def lower_body(source, out, work, panel, sem, *, count, size):
    copy = pltpu.make_async_copy(source, work, sem)
    copy.start()
    copy.wait()
    factor_steps(work, panel, out, lambda k: None, count=count, size=size)


def lower_factors(blocks):
    count, size, _ = blocks.shape
    return pl.pallas_call(
        functools.partial(lower_body, count=count, size=size),
        out_shape=jax.ShapeDtypeStruct(blocks.shape, jnp.float32),
        in_specs=[pl.BlockSpec(memory_space=pl.ANY)],
        out_specs=pl.BlockSpec(memory_space=pltpu.VMEM),
        scratch_shapes=[
            pltpu.VMEM(blocks.shape, jnp.float32),
            pltpu.VMEM((count, TILE, 2 * TILE), jnp.float32),
            pltpu.SemaphoreType.DMA,
        ],
        compiler_params=pltpu.CompilerParams(vmem_limit_bytes=48 * MIB),
        name="lower_factors",
    )(blocks)


def wide_shards(points, freqs, phase, ridge, targets):
    data_count = lax.axis_size("dp")
    feat_count = lax.axis_size("feat")
    feat_index = lax.axis_index("feat")
    data_index = lax.axis_index("dp")
    local_width = freqs.shape[1]
    total_width = local_width * feat_count
    tile_width = total_width // data_count
    window = max(local_width, FB)
    window_start = feat_index * local_width // window * window
    row_start = feat_index * local_width
    col_start = data_index * tile_width
    scale = math.sqrt(2.0 / (points.shape[0] * data_count))
    points_all = lax.all_gather(points, "dp", axis=0, tiled=True)
    targets_all = lax.all_gather(targets, "dp", axis=1, tiled=True)
    freqs_all = lax.all_gather(freqs, "feat", axis=1, tiled=True)
    turns = phase * (0.5 / math.pi)
    turns_all, ridge_all = lax.all_gather(jnp.stack([turns, ridge]), "feat", axis=1, tiled=True)

    def features_at(start, width):
        return features(
            points_all,
            lax.dynamic_slice_in_dim(freqs_all, start, width, 1),
            lax.dynamic_slice_in_dim(turns_all, start, width, 0),
            scale,
        )

    window_phi = features_at(window_start, window)
    row_phi = lax.dynamic_slice_in_dim(window_phi, row_start - window_start, local_width, 1)
    window_ridge = lax.dynamic_slice_in_dim(ridge_all, window_start, window, 0)
    blocks = []
    for first in range(0, window, FB):
        part = window_phi[:, first : first + FB]
        block_ridge = window_ridge[first : first + FB, None]
        blocks.append(with_ridge(cross(part, part), block_ridge, 0, 0))
    factors_all = lower_factors(jnp.stack(blocks)).reshape(window, FB)
    factor_rows = lax.dynamic_slice_in_dim(factors_all, row_start - window_start, local_width, 0)
    col_phi = features_at(col_start, tile_width)
    gram_part = with_ridge(cross(row_phi, col_phi), ridge[:, None], row_start, col_start)
    projected = jnp.dot(targets_all, row_phi, preferred_element_type=jnp.float32)
    return gram_part, projected, factor_rows


def shards(points, freqs, phase, ridge, targets):
    local_width = freqs.shape[1]
    data_count, feat_count = lax.axis_size("dp"), lax.axis_size("feat")
    tile_width = local_width * feat_count // data_count
    near = (
        local_width % FB == 0
        and local_width % tile_width == 0
        and tile_width % WIDE == 0
        and data_count % 2 == 0
        and feat_count == 4
    )
    return (near_shards if near else wide_shards)(points, freqs, phase, ridge, targets)


def solution(mesh):
    in_specs = (P("dp", None), P(None, "feat"), P("feat"), P("feat"), P(None, "dp"))
    out_specs = (P("feat", "dp"), P(None, "feat"), P("feat", None))
    return jax.shard_map(shards, mesh=mesh, in_specs=in_specs, out_specs=out_specs, check_vma=False)
```

profile of v0, /device:TPU:18, one launch (start us, length us, event | category | flops | bytes accessed | tf_op | source)
XLA Modules:
  0.0 100.6 jit_solution(8131716762777816732)
XLA Ops:
  0.6 0.7 dynamic-slice.3
  1.3 0.0 copy-start.1
  1.3 1.2 %copy-done.1 = bf16[256,2048]{1,0:T(8,128)(2,1)S(1)} copy-done((bf16[256,2048]{1,0:T(8,128)(2,1)S(1)}, bf16[256,2048]{1,0:T(8,128)(2,1)}, u32[]{:S(2)}) %copy-start.1) | copy-done | bytes 1048600
  2.6 0.0 copy-start.2
  2.6 0.9 copy-done.2
  3.5 0.0 copy-start.3
  3.5 0.7 copy-done.3
  4.2 0.0 copy-start.4
  4.2 0.7 copy-done.4
  4.8 32.0 %spread.1 = (bf16[2048,2048]{1,0:T(8,128)(2,1)S(1)}, bf16[2048,256]{1,0:T(8,128)(2,1)S(1)}, bf16[256,1024]{1,0:T(8,128)(2,1)S(1)}, f32[4,1,2048]{2,1,0:T(1,128)S(1)}, f32[8,2048]{1,0:T(8,128)S(1)}) custom-call(bf16[256,256]{1,0:T(8,128)(2,1)S(1)} %copy-done.2, bf16[8,256]{1,0:T(8,128)(2,1)S(1)} %copy-done.4, f32[1,2048]{1,0:T(1,128)S(1)} %bitcast.9, ...), custom_call_target="tpu_custom_call" | custom-call | flops 2147483648 | bytes 8388608 | tf_op jit(solution)/shard_map/spread/pallas_call | solution.py:340
  36.9 0.0 copy-start
  36.9 18.5 %gram_tile.1 = f32[2048,1024]{1,0:T(8,128)} custom-call(bf16[2048,2048]{1,0:T(8,128)(2,1)S(1)} %get-tuple-element.10.phi, bf16[2048,256]{1,0:T(8,128)(2,1)S(1)} %get-tuple-element.11.points, bf16[256,1024]{1,0:T(8,128)(2,1)S(1)} %get-tuple-element.12.freqs, f32[1,1024]{1,0:T(1,128)S(1)} %constant_dynamic-slice_fusion.phase, f32[1,1024]{1,0:T(1,128)S(1)} %bitcast.6, ...), custom_call_target="tpu_custom_call" | custom-call | flops 8589934592 | bytes 8388608 | tf_op jit(solution)/shard_map/gram_tile/pallas_call | solution.py:487
  55.4 0.0 copy-done
  55.4 45.1 %lower_factors.1 = (f32[2,1024,1024]{2,1,0:T(8,128)}, f32[8,2048]{1,0:T(8,128)}) custom-call(bf16[2048,2048]{1,0:T(8,128)(2,1)S(1)} %get-tuple-element.10.phi, f32[8,2048]{1,0:T(8,128)S(1)} %get-tuple-element.14.sums, f32[1,2048]{1,0:T(1,128)S(1)} %bitcast.7), custom_call_target="tpu_custom_call" | custom-call | flops 128849018880 | bytes 33554432 | tf_op jit(solution)/shard_map/lower_factors/pallas_call | solution.py:411
  (1 shorter events, 0.0 us)
Async XLA Ops:
  1.3 1.2 %copy-start.1 = (bf16[256,2048]{1,0:T(8,128)(2,1)S(1)}, bf16[256,2048]{1,0:T(8,128)(2,1)}, u32[]{:S(2)}) copy-start(bf16[256,2048]{1,0:T(8,128)(2,1)} %freqs.1) | copy-start | bytes 3145732
  2.6 0.9 copy-start.2
  3.5 0.7 copy-start.3
  4.2 0.7 copy-start.4
  36.9 18.6 %copy-start = (f32[2048]{0:T(1024)S(1)}, f32[2048]{0:T(1024)}, u32[]{:S(2)}) copy-start(f32[2048]{0:T(1024)} %param.8) | copy-start | bytes 24580
where the time goes:
time: 101 us
  Pallas kernels  95.6 us (95%)
  local copies, waits for them, and re-layouts  4.22 us (4%)
    pallas_call x1, Pallas kernels, factor(): pl.pallas_call(functools.partial(factor_body, count=count, size=size), ou...  45.1 us
    pallas_call x1, Pallas kernels, spread(): pl.pallas_call(functools.partial(spread_body, data_count=data_count, feat...  32 us
    pallas_call x1, Pallas kernels, gram_tile(): pl.pallas_call(functools.partial(tile_body, scale=scale), out_shape=jax.S...  18.5 us
    unnamed x10, local copies, waits for them, and re-layouts  3.52 us

commit v1 on v0

--- a/solution.py
+++ b/solution.py
@@ -12,6 +12,9 @@
 TILE = 128
 MICRO = 16
 WIDE = 256
+BAND = 32
+SUBLANES = 8
+HALF = TILE // 2
 MIB = 1024 * 1024
 COS_TURNS = (
     0.9999991998413438,
@@ -82,6 +85,140 @@
         rows_lead = jnp.where(here, lead, rows_lead - below * lead)
         rows_tail = jnp.where(here, tail, rows_tail - below * tail)
     return rows_lead, rows_tail
+
+
+def spread_row(value, row):
+    return jnp.broadcast_to(value[row : row + 1, :], value.shape)
+
+
+def pair_rows(groups, own, base):
+    shape = (SUBLANES, TILE)
+    row_ids = lax.broadcasted_iota(jnp.int32, shape, 0)
+    lanes = lax.broadcasted_iota(jnp.int32, shape, 1)
+    side = jnp.where(lanes < HALF, base, base + HALF)
+    count = len(groups)
+    size = count * SUBLANES
+    cols = [
+        {
+            g: jnp.take_along_axis(groups[g][own], side + m, axis=1)
+            for g in range(m // SUBLANES, count)
+        }
+        for m in range(size)
+    ]
+    pivot = spread_row(cols[0][0], 0)
+    for i in range(size):
+        gi, ri = divmod(i, SUBLANES)
+        inv = lax.rsqrt(pivot)
+        if i + 1 < size:
+            gn, rn = divmod(i + 1, SUBLANES)
+            step = spread_row(cols[i][gn], rn) * inv
+            pivot = spread_row(cols[i + 1][gn], rn) - step * step
+        mult = {g: cols[i][g] * inv for g in range(gi, count)}
+        for m in range(i + 1, size):
+            gm, rm = divmod(m, SUBLANES)
+            scalar = spread_row(mult[gm], rm)
+            for g in range(gm, count):
+                cols[m][g] = cols[m][g] - mult[g] * scalar
+        below = jnp.where(row_ids > ri, mult[gi], 0.0)
+        here = row_ids == ri
+        for x in range(len(groups[0])):
+            lead = spread_row(groups[gi][x], ri) * inv
+            groups[gi][x] = jnp.where(here, lead, groups[gi][x] - below * lead)
+            for g in range(gi + 1, count):
+                groups[g][x] = groups[g][x] - mult[g] * lead
+    return groups
+
+
+def pair_panel(panel, beside):
+    low = lax.broadcasted_iota(jnp.int32, (HALF, TILE), 1) < HALF
+    for start in range(0, TILE, BAND):
+        end = start + BAND
+        beside(start // BAND)
+        quarter = start // HALF
+        parts = range(quarter, quarter + 3)
+        groups = [
+            [panel[x, r : r + SUBLANES, :] for x in parts]
+            for r in range(start, end, SUBLANES)
+        ]
+        groups = pair_rows(groups, 0, start % HALF)
+        for g, group in enumerate(groups):
+            for x, value in zip(parts, group):
+                panel[x, start + g * SUBLANES : start + (g + 1) * SUBLANES, :] = value
+        bands = [jnp.concatenate([group[x] for group in groups], axis=0) for x in range(3)]
+        right = right_parts(jnp.concatenate(bands, axis=1))
+        for q in range(end // HALF, TILE // HALF):
+            first = max(end - q * HALF, 0)
+            update = cross(left_parts(bands[q - quarter], 0), right)
+            for x in parts:
+                at = (x - quarter) * TILE
+                piece = jnp.where(
+                    low[first:],
+                    update[first:HALF, at : at + TILE],
+                    update[HALF + first :, at : at + TILE],
+                )
+                rows = slice(q * HALF + first, (q + 1) * HALF)
+                panel[x, rows, :] = panel[x, rows, :] - piece
+
+
+def pair_steps(work, packed, panel, out, begin, beside, emit, *, size):
+    tiles = size // TILE
+    row_ids = lax.broadcasted_iota(jnp.int32, (TILE, TILE), 0)
+    col_ids = lax.broadcasted_iota(jnp.int32, (TILE, TILE), 1)
+    low = col_ids < HALF
+
+    def swap(left, right):
+        return (
+            jnp.where(low, left, pltpu.roll(right, HALF, 1)),
+            jnp.where(low, pltpu.roll(left, HALF, 1), right),
+        )
+
+    def step(k, carry):
+        begin(k)
+        at = pl.multiple_of(k * TILE, TILE)
+        diagonal = [work[blk, pl.ds(at, TILE), pl.ds(at, TILE)] for blk in range(2)]
+        packed[0], packed[1] = swap(*diagonal)
+        packed[2] = jnp.where(row_ids == lax.rem(col_ids, HALF), 1.0, 0.0)
+        packed[3] = jnp.where(row_ids == lax.rem(col_ids, HALF) + HALF, 1.0, 0.0)
+        pair_panel(packed, functools.partial(beside, k))
+        lead = swap(packed[0], packed[1])
+        tail = swap(packed[2], packed[3])
+        for blk in range(2):
+            panel[blk] = tail[blk]
+            lower = jnp.where(row_ids >= col_ids, lead[blk].T, 0.0)
+            out[blk, pl.ds(at, TILE), pl.ds(at, TILE)] = lower
+        for c in range(tiles - 1):
+
+            @pl.when(k == c)
+            def _():
+                trailing(work, panel, out, c, 2, size)
+
+        emit(k)
+        return carry
+
+    lax.fori_loop(0, tiles, step, 0)
+
+
+def trailing(work, panel, out, c, count, size):
+    lo, mid = c * TILE, (c + 1) * TILE
+    for blk in range(count):
+        upper = jnp.dot(
+            left_parts(panel[blk], 1),
+            right_parts(work[blk, lo:mid, mid:]),
+            preferred_element_type=jnp.float32,
+        )
+        lower = upper.T
+        out[blk, mid:, lo:mid] = lower
+        out[blk, lo:mid, mid:] = jnp.zeros_like(upper)
+        left = left_parts(lower, 1)
+        right = right_parts(upper)
+        rest = size - mid
+        for first in range(0, rest, 2 * TILE):
+            last = min(first + 2 * TILE, rest)
+            update = jnp.dot(
+                left[first:last], right[:, first:], preferred_element_type=jnp.float32
+            )
+            r = mid + first
+            work[blk, r : mid + last, r:] = work[blk, r : mid + last, r:] - update
 
 
 def factor_steps(work, panel, out, emit, *, count, size):
@@ -280,11 +417,11 @@
         targets_wait(other)
         compute(other)
 
-        @pl.when((side_x + side_y == 1) & (t >= chips - half))
+        @pl.when((side_x + side_y == 1) & (t <= half))
         def _():
-            q = side_y * half + t - (chips - half)
+            q = side_y * half + t - 1
             freqs_pass(q, 0).wait_recv()
-            freqs_pass(q, t - (chips - half)).start()
+            freqs_pass(q, t - 1).start()
 
         return carry
 
@@ -379,9 +516,30 @@
     )(points, targets, phase[None, :], freqs)
 
 
-def factor_body(phi, sums, ridge, out, projected, work, block_out, panel, out_sem,
-                *, count, size):
+def assemble_body(phi, sums, ridge, points, freqs, phase, col_ridge, start, out, projected, gram,
+                  work, block_out, packed, panel, cols_phi, ring, out_sem, ring_sem,
+                  *, count, size, scale):
     projected[...] = sums[...]
+    width, rows = phi.shape
+    columns = freqs.shape[1]
+    bands = TILE // BAND
+    wide, down = columns // WIDE, width // WIDE
+    parts = down // bands
+    chunk = rows // down
+    tall = bands * WIDE
+
+    def make(j, r):
+        cols = pl.ds(pl.multiple_of(j * WIDE, WIDE), WIDE)
+        at = pl.ds(pl.multiple_of(r * chunk, chunk), chunk)
+        cols_phi[lax.rem(j, 2), at, :] = features(
+            points[at, :], freqs[:, cols], phase[:, cols], scale
+        )
+
+    def first(r, carry):
+        make(0, r)
+        return carry
+
+    lax.fori_loop(0, down, first, 0)
     for blk in range(count):
         base = blk * size
         for c in range(0, size, WIDE):
@@ -393,113 +551,87 @@
         at = pl.ds(pl.multiple_of(k * TILE, TILE), TILE)
         return pltpu.make_async_copy(block_out.at[blk, at], out.at[blk, at], out_sem.at[blk])
 
+    def place(k):
+        return k // parts, lax.rem(k, parts)
+
+    def ring_out(k):
+        j, part = place(k)
+        slot = lax.rem(k, 2)
+        return pltpu.make_async_copy(
+            ring.at[slot],
+            gram.at[pl.ds(pl.multiple_of(part * tall, tall), tall),
+                    pl.ds(pl.multiple_of(j * WIDE, WIDE), WIDE)],
+            ring_sem.at[slot])
+
+    def begin(k):
+        @pl.when(k >= 2)
+        def _():
+            ring_out(k).wait()
+
+    def beside(k, band):
+        j, part = place(k)
+        r = part * bands + band
+        at = pl.ds(pl.multiple_of(r * WIDE, WIDE), WIDE)
+        ring[lax.rem(k, 2), band * WIDE : (band + 1) * WIDE, :] = jnp.dot(
+            phi[at, :], cols_phi[lax.rem(j, 2)], preferred_element_type=jnp.float32
+        )
+        make(lax.rem(j + 1, wide), r)
+
     def emit(k):
+        j, part = place(k)
+        shift = start[0] + j * WIDE - part * tall
+
+        @pl.when((shift >= 0) & (shift < tall))
+        def _():
+            at = pl.ds(pl.multiple_of(shift, WIDE), WIDE)
+            cols = pl.ds(pl.multiple_of(j * WIDE, WIDE), WIDE)
+            slot = lax.rem(k, 2)
+            ring[slot, at, :] = with_ridge(ring[slot, at, :], col_ridge[:, cols], 0, 0)
+
+        ring_out(k).start()
         for blk in range(count):
             rows_out(blk, k).start()
 
-    factor_steps(work, panel, block_out, emit, count=count, size=size)
+    pair_steps(work, packed, panel, block_out, begin, beside, emit, size=size)
+    tiles = size // TILE
+    for k in range(tiles - 2, tiles):
+        ring_out(k).wait()
     for blk in range(count):
         pltpu.make_async_copy(block_out.at[blk], out.at[blk], out_sem.at[blk]).wait()
 
 
-def factor(phi, sums, ridge, size):
+def assemble(phi, sums, ridge, points, freqs, phase, col_ridge, start, size, scale):
     width, rows = phi.shape
+    columns = freqs.shape[1]
     count = width // size
     outs = sums.shape[0]
     vmem = pl.BlockSpec(memory_space=pltpu.VMEM)
     hbm = pl.BlockSpec(memory_space=pltpu.HBM)
     return pl.pallas_call(
-        functools.partial(factor_body, count=count, size=size),
+        functools.partial(assemble_body, count=count, size=size, scale=scale),
         out_shape=(
             jax.ShapeDtypeStruct((count, size, size), jnp.float32),
             jax.ShapeDtypeStruct((outs, width), jnp.float32),
+            jax.ShapeDtypeStruct((width, columns), jnp.float32),
         ),
-        in_specs=[vmem] * 3,
-        out_specs=(hbm, vmem),
+        in_specs=[vmem] * 7 + [pl.BlockSpec(memory_space=pltpu.SMEM)],
+        out_specs=(hbm, vmem, hbm),
         scratch_shapes=[
             pltpu.VMEM((count, size, size), jnp.float32),
             pltpu.VMEM((count, size, size), jnp.float32),
-            pltpu.VMEM((count, TILE, 2 * TILE), jnp.float32),
+            pltpu.VMEM((4, TILE, TILE), jnp.float32),
+            pltpu.VMEM((count, TILE, TILE), jnp.float32),
+            pltpu.VMEM((2, rows, WIDE), jnp.bfloat16),
+            pltpu.VMEM((2, TILE // BAND * WIDE, WIDE), jnp.float32),
             pltpu.SemaphoreType.DMA((count,)),
+            pltpu.SemaphoreType.DMA((2,)),
         ],
-        compiler_params=pltpu.CompilerParams(vmem_limit_bytes=32 * MIB),
+        compiler_params=pltpu.CompilerParams(vmem_limit_bytes=40 * MIB),
         cost_estimate=pl.CostEstimate(
             flops=30 * rows * width * size, bytes_accessed=8 * rows * width, transcendentals=0
         ),
-        name="lower_factors",
-    )(phi, sums, ridge)
-
-
-def tile_body(phi, points, freqs, phase, ridge, start, out, cols_phi, ring, out_sem, *, scale):
-    width, rows = phi.shape
-    columns = freqs.shape[1]
-    slots, tall, _ = ring.shape
-    down, wide = width // tall, columns // WIDE
-    chunk = rows // down
-
-    def make(j, r):
-        cols = pl.ds(pl.multiple_of(j * WIDE, WIDE), WIDE)
-        at = pl.ds(pl.multiple_of(r * chunk, chunk), chunk)
-        cols_phi[lax.rem(j, 2), at, :] = features(
-            points[at, :], freqs[:, cols], phase[:, cols], scale
-        )
-
-    def store(j, r, slot):
-        return pltpu.make_async_copy(
-            ring.at[slot],
-            out.at[pl.ds(pl.multiple_of(r * tall, tall), tall),
-                   pl.ds(pl.multiple_of(j * WIDE, WIDE), WIDE)],
-            out_sem.at[slot])
-
-    def first(r, carry):
-        make(0, r)
-        return carry
-
-    lax.fori_loop(0, down, first, 0)
-
-    def one(it, carry):
-        j, r = it // down, lax.rem(it, down)
-        slot = lax.rem(it, slots)
-
-        @pl.when(it >= slots)
-        def _():
-            store(j, r, slot).wait()
-
-        cols = pl.ds(pl.multiple_of(j * WIDE, WIDE), WIDE)
-        at = pl.ds(pl.multiple_of(r * tall, tall), tall)
-        tile = jnp.dot(phi[at, :], cols_phi[lax.rem(j, 2)], preferred_element_type=jnp.float32)
-        ring[slot] = with_ridge(tile, ridge[:, cols], r * tall, j * WIDE + start[0])
-        make(lax.rem(j + 1, wide), r)
-        store(j, r, slot).start()
-        return carry
-
-    total = down * wide
-    lax.fori_loop(0, total, one, 0)
-    for it in range(total - slots, total):
-        store(it // down, it % down, it % slots).wait()
-
-
-def gram_tile(phi, points, freqs, phase, ridge, start, scale):
-    width, rows = phi.shape
-    columns = freqs.shape[1]
-    vmem = pl.BlockSpec(memory_space=pltpu.VMEM)
-    slots = 3
-    return pl.pallas_call(
-        functools.partial(tile_body, scale=scale),
-        out_shape=jax.ShapeDtypeStruct((width, columns), jnp.float32),
-        in_specs=[vmem, vmem, vmem, vmem, vmem, pl.BlockSpec(memory_space=pltpu.SMEM)],
-        out_specs=pl.BlockSpec(memory_space=pltpu.HBM),
-        scratch_shapes=[
-            pltpu.VMEM((2, rows, WIDE), jnp.bfloat16),
-            pltpu.VMEM((slots, 2 * WIDE, WIDE), jnp.float32),
-            pltpu.SemaphoreType.DMA((slots,)),
-        ],
-        compiler_params=pltpu.CompilerParams(vmem_limit_bytes=24 * MIB),
-        cost_estimate=pl.CostEstimate(
-            flops=2 * rows * width * columns, bytes_accessed=4 * width * columns, transcendentals=0
-        ),
-        name="gram_tile",
-    )(phi, points, freqs, phase, ridge, start)
+        name="assemble",
+    )(phi, sums, ridge, points, freqs, phase, col_ridge, start)
 
 
 def near_shards(points, freqs, phase, ridge, targets):
@@ -511,12 +643,14 @@
     phi, points_all, col_freqs, turns, sums = spread(
         points, targets, phase, freqs, tile_width, scale
     )
-    factors, projected = factor(phi, sums, ridge[None, :], FB)
     col_start = data_index * tile_width
     start = col_start - feat_index * local_width
     col_turns = lax.dynamic_slice_in_dim(turns.reshape(1, -1), col_start, tile_width, 1)
     col_ridge = lax.dynamic_slice_in_dim(ridge[None, :], start, tile_width, 1)
-    gram = gram_tile(phi, points_all, col_freqs, col_turns, col_ridge, start[None], scale)
+    factors, projected, gram = assemble(
+        phi, sums, ridge[None, :], points_all, col_freqs, col_turns, col_ridge, start[None],
+        FB, scale,
+    )
     return gram, projected, factors.reshape(local_width, FB)
 
 
@@ -592,9 +726,11 @@
     data_count, feat_count = lax.axis_size("dp"), lax.axis_size("feat")
     tile_width = local_width * feat_count // data_count
     near = (
-        local_width % FB == 0
+        local_width == 2 * FB
         and local_width % tile_width == 0
         and tile_width % WIDE == 0
+        and tile_width // WIDE * (local_width // WIDE) == FB // BAND
+        and points.shape[0] * data_count % (local_width // WIDE) == 0
         and data_count % 2 == 0
         and feat_count == 4
     )

time: 101 us -> 83.4 us (0.83)
  Pallas kernels: 95.6 us -> 77.3 us
    pallas_call x2 -> x1, Pallas kernels: 63.6 us -> 48.9 us  [assemble(): pl.pallas_call(functools.partial(assemble_body, count=count, size=size, s...]
    pallas_call x1, Pallas kernels: 32 us -> 28.5 us  [spread(): pl.pallas_call(functools.partial(spread_body, data_count=data_count, feat...]
where the time goes in v1:
time: 83.4 us; the launch traced here: 83.1 us
  Pallas kernels  77.3 us (93%)
  local copies, waits for them, and re-layouts  4.91 us (6%)
    pallas_call x1, Pallas kernels, assemble(): pl.pallas_call(functools.partial(assemble_body, count=count, size=size, s...  48.9 us
    pallas_call x1, Pallas kernels, spread(): pl.pallas_call(functools.partial(spread_body, data_count=data_count, feat...  28.5 us
    unnamed x10, local copies, waits for them, and re-layouts  4.2 us

profile of v1, /device:TPU:18, one launch (start us, length us, event | category | flops | bytes accessed | tf_op | source)
XLA Modules:
  0.0 83.1 jit_solution(4880215042841600604)
XLA Ops:
  0.6 0.7 dynamic-slice.3
  1.3 0.0 copy-start.1
  1.3 1.2 %copy-done.1 = bf16[256,2048]{1,0:T(8,128)(2,1)S(1)} copy-done((bf16[256,2048]{1,0:T(8,128)(2,1)S(1)}, bf16[256,2048]{1,0:T(8,128)(2,1)}, u32[]{:S(2)}) %copy-start.1) | copy-done | bytes 1048600
  2.6 0.0 copy-start.2
  2.6 0.9 %copy-done.2 = bf16[256,256]{1,0:T(8,128)(2,1)S(1)} copy-done((bf16[256,256]{1,0:T(8,128)(2,1)S(1)}, bf16[256,256]{1,0:T(8,128)(2,1)}, u32[]{:S(2)}) %copy-start.2) | copy-done | bytes 131096
  3.5 0.0 copy-start.3
  3.5 0.7 copy-done.3
  4.2 0.0 copy-start.4
  4.2 0.7 copy-done.4
  4.8 28.5 %spread.1 = (bf16[2048,2048]{1,0:T(8,128)(2,1)S(1)}, bf16[2048,256]{1,0:T(8,128)(2,1)S(1)}, bf16[256,1024]{1,0:T(8,128)(2,1)S(1)}, f32[4,1,2048]{2,1,0:T(1,128)S(1)}, f32[8,2048]{1,0:T(8,128)S(1)}) custom-call(bf16[256,256]{1,0:T(8,128)(2,1)S(1)} %copy-done.2, bf16[8,256]{1,0:T(8,128)(2,1)S(1)} %copy-done.4, f32[1,2048]{1,0:T(1,128)S(1)} %bitcast.9, ...), custom_call_target="tpu_custom_call" | custom-call | flops 2147483648 | bytes 8388608 | tf_op jit(solution)/shard_map/spread/pallas_call | solution.py:477
  33.3 0.0 copy-start
  33.4 0.7 copy-done
  34.0 48.9 %assemble.1 = (f32[2,1024,1024]{2,1,0:T(8,128)}, f32[8,2048]{1,0:T(8,128)}, f32[2048,1024]{1,0:T(8,128)}) custom-call(bf16[2048,2048]{1,0:T(8,128)(2,1)S(1)} %get-tuple-element.11.phi, f32[8,2048]{1,0:T(8,128)S(1)} %get-tuple-element.12.sums, f32[1,2048]{1,0:T(1,128)S(1)} %bitcast.7, bf16[2048,256]{1,0:T(8,128)(2,1)S(1)} %get-tuple-element.13.points, ...), custom_call_target="tpu_custom_call" | custom-call | flops 128849018880 | bytes 33554432 | tf_op jit(solution)/shard_map/assemble/pallas_call | solution.py:610
  (1 shorter events, 0.0 us)
Async XLA Ops:
  1.3 1.2 %copy-start.1 = (bf16[256,2048]{1,0:T(8,128)(2,1)S(1)}, bf16[256,2048]{1,0:T(8,128)(2,1)}, u32[]{:S(2)}) copy-start(bf16[256,2048]{1,0:T(8,128)(2,1)} %freqs.1) | copy-start | bytes 3145732
  2.6 0.9 %copy-start.2 = (bf16[256,256]{1,0:T(8,128)(2,1)S(1)}, bf16[256,256]{1,0:T(8,128)(2,1)}, u32[]{:S(2)}) copy-start(bf16[256,256]{1,0:T(8,128)(2,1)} %points.1) | copy-start | bytes 393220
  3.5 0.7 copy-start.3
  4.2 0.7 copy-start.4
  33.3 0.7 copy-start

commit v2 on v1

--- a/solution.py
+++ b/solution.py
@@ -13,6 +13,7 @@
 MICRO = 16
 WIDE = 256
 BAND = 32
+SUBBAND = 16
 SUBLANES = 8
 HALF = TILE // 2
 MIB = 1024 * 1024
@@ -98,34 +99,36 @@
     side = jnp.where(lanes < HALF, base, base + HALF)
     count = len(groups)
     size = count * SUBLANES
-    cols = [
-        {
-            g: jnp.take_along_axis(groups[g][own], side + m, axis=1)
-            for g in range(m // SUBLANES, count)
+    for first in range(0, size, SUBBAND):
+        span = range(first, first + SUBBAND)
+        cols = {
+            m: {
+                g: jnp.take_along_axis(groups[g][own], side + m, axis=1)
+                for g in range(m // SUBLANES, count)
+            }
+            for m in span
         }
-        for m in range(size)
-    ]
-    pivot = spread_row(cols[0][0], 0)
-    for i in range(size):
-        gi, ri = divmod(i, SUBLANES)
-        inv = lax.rsqrt(pivot)
-        if i + 1 < size:
-            gn, rn = divmod(i + 1, SUBLANES)
-            step = spread_row(cols[i][gn], rn) * inv
-            pivot = spread_row(cols[i + 1][gn], rn) - step * step
-        mult = {g: cols[i][g] * inv for g in range(gi, count)}
-        for m in range(i + 1, size):
-            gm, rm = divmod(m, SUBLANES)
-            scalar = spread_row(mult[gm], rm)
-            for g in range(gm, count):
-                cols[m][g] = cols[m][g] - mult[g] * scalar
-        below = jnp.where(row_ids > ri, mult[gi], 0.0)
-        here = row_ids == ri
-        for x in range(len(groups[0])):
-            lead = spread_row(groups[gi][x], ri) * inv
-            groups[gi][x] = jnp.where(here, lead, groups[gi][x] - below * lead)
-            for g in range(gi + 1, count):
-                groups[g][x] = groups[g][x] - mult[g] * lead
+        pivot = spread_row(cols[first][first // SUBLANES], first % SUBLANES)
+        for i in span:
+            gi, ri = divmod(i, SUBLANES)
+            inv = lax.rsqrt(pivot)
+            if i + 1 in span:
+                gn, rn = divmod(i + 1, SUBLANES)
+                step = spread_row(cols[i][gn], rn) * inv
+                pivot = spread_row(cols[i + 1][gn], rn) - step * step
+            mult = {g: cols[i][g] * inv for g in range(gi, count)}
+            for m in range(i + 1, span.stop):
+                gm, rm = divmod(m, SUBLANES)
+                scalar = spread_row(mult[gm], rm)
+                for g in range(gm, count):
+                    cols[m][g] = cols[m][g] - mult[g] * scalar
+            below = jnp.where(row_ids > ri, mult[gi], 0.0)
+            here = row_ids == ri
+            for x in range(len(groups[0])):
+                lead = spread_row(groups[gi][x], ri) * inv
+                groups[gi][x] = jnp.where(here, lead, groups[gi][x] - below * lead)
+                for g in range(gi + 1, count):
+                    groups[g][x] = groups[g][x] - mult[g] * lead
     return groups
 
 
@@ -516,7 +519,7 @@
     )(points, targets, phase[None, :], freqs)
 
 
-def assemble_body(phi, sums, ridge, points, freqs, phase, col_ridge, start, out, projected, gram,
+def assemble_body(phi, sums, ridge, points, freqs, phases, out, projected, gram,
                   work, block_out, packed, panel, cols_phi, ring, out_sem, ring_sem,
                   *, count, size, scale):
     projected[...] = sums[...]
@@ -527,12 +530,17 @@
     parts = down // bands
     chunk = rows // down
     tall = bands * WIDE
+    col_start = lax.axis_index("dp") * columns
+    start = col_start - lax.axis_index("feat") * width
+    holder = col_start // width
+    offset = lax.rem(col_start, width)
 
     def make(j, r):
         cols = pl.ds(pl.multiple_of(j * WIDE, WIDE), WIDE)
         at = pl.ds(pl.multiple_of(r * chunk, chunk), chunk)
         cols_phi[lax.rem(j, 2), at, :] = features(
-            points[at, :], freqs[:, cols], phase[:, cols], scale
+            points[at, :], freqs[:, cols],
+            phases[holder, :, pl.ds(pl.multiple_of(offset + j * WIDE, WIDE), WIDE)], scale
         )
 
     def first(r, carry):
@@ -579,14 +587,14 @@
 
     def emit(k):
         j, part = place(k)
-        shift = start[0] + j * WIDE - part * tall
+        shift = start + j * WIDE - part * tall
 
         @pl.when((shift >= 0) & (shift < tall))
         def _():
             at = pl.ds(pl.multiple_of(shift, WIDE), WIDE)
-            cols = pl.ds(pl.multiple_of(j * WIDE, WIDE), WIDE)
+            cols = pl.ds(pl.multiple_of(start + j * WIDE, WIDE), WIDE)
             slot = lax.rem(k, 2)
-            ring[slot, at, :] = with_ridge(ring[slot, at, :], col_ridge[:, cols], 0, 0)
+            ring[slot, at, :] = with_ridge(ring[slot, at, :], ridge[:, cols], 0, 0)
 
         ring_out(k).start()
         for blk in range(count):
@@ -600,7 +608,7 @@
         pltpu.make_async_copy(block_out.at[blk], out.at[blk], out_sem.at[blk]).wait()
 
 
-def assemble(phi, sums, ridge, points, freqs, phase, col_ridge, start, size, scale):
+def assemble(phi, sums, ridge, points, freqs, phases, size, scale):
     width, rows = phi.shape
     columns = freqs.shape[1]
     count = width // size
@@ -614,7 +622,7 @@
             jax.ShapeDtypeStruct((outs, width), jnp.float32),
             jax.ShapeDtypeStruct((width, columns), jnp.float32),
         ),
-        in_specs=[vmem] * 7 + [pl.BlockSpec(memory_space=pltpu.SMEM)],
+        in_specs=[vmem] * 6,
         out_specs=(hbm, vmem, hbm),
         scratch_shapes=[
             pltpu.VMEM((count, size, size), jnp.float32),
@@ -626,30 +634,24 @@
             pltpu.SemaphoreType.DMA((count,)),
             pltpu.SemaphoreType.DMA((2,)),
         ],
-        compiler_params=pltpu.CompilerParams(vmem_limit_bytes=40 * MIB),
+        compiler_params=pltpu.CompilerParams(vmem_limit_bytes=36 * MIB),
         cost_estimate=pl.CostEstimate(
             flops=30 * rows * width * size, bytes_accessed=8 * rows * width, transcendentals=0
         ),
         name="assemble",
-    )(phi, sums, ridge, points, freqs, phase, col_ridge, start)
+    )(phi, sums, ridge, points, freqs, phases)
 
 
 def near_shards(points, freqs, phase, ridge, targets):
     data_count, feat_count = lax.axis_size("dp"), lax.axis_size("feat")
-    data_index, feat_index = lax.axis_index("dp"), lax.axis_index("feat")
     local_width = freqs.shape[1]
     tile_width = local_width * feat_count // data_count
     scale = math.sqrt(2.0 / (points.shape[0] * data_count))
     phi, points_all, col_freqs, turns, sums = spread(
         points, targets, phase, freqs, tile_width, scale
     )
-    col_start = data_index * tile_width
-    start = col_start - feat_index * local_width
-    col_turns = lax.dynamic_slice_in_dim(turns.reshape(1, -1), col_start, tile_width, 1)
-    col_ridge = lax.dynamic_slice_in_dim(ridge[None, :], start, tile_width, 1)
     factors, projected, gram = assemble(
-        phi, sums, ridge[None, :], points_all, col_freqs, col_turns, col_ridge, start[None],
-        FB, scale,
+        phi, sums, ridge[None, :], points_all, col_freqs, turns, FB, scale
     )
     return gram, projected, factors.reshape(local_width, FB)
 

time: 83.4 us -> 78.3 us (0.939)
  Pallas kernels: 77.3 us -> 73 us
    pallas_call x1, Pallas kernels: 48.9 us -> 44.5 us  [assemble(): pl.pallas_call(functools.partial(assemble_body, count=count, size=size, s...]
where the time goes in v2:
time: 78.3 us; the launch traced here: 78 us
  Pallas kernels  73 us (93%)
  local copies, waits for them, and re-layouts  4.2 us (5%)
  between operations  0.82 us (1%)
    pallas_call x1, Pallas kernels, assemble(): pl.pallas_call(functools.partial(assemble_body, count=count, size=size, s...  44.5 us
    pallas_call x1, Pallas kernels, spread(): pl.pallas_call(functools.partial(spread_body, data_count=data_count, feat...  28.5 us
    unnamed x10, local copies, waits for them, and re-layouts  4.2 us

profile of v2, /device:TPU:18, one launch (start us, length us, event | category | flops | bytes accessed | tf_op | source)
XLA Modules:
  0.0 78.0 jit_solution(16737320946949802657)
XLA Ops:
  0.6 0.0 copy-start
  0.6 1.2 %copy-done = bf16[256,2048]{1,0:T(8,128)(2,1)S(1)} copy-done((bf16[256,2048]{1,0:T(8,128)(2,1)S(1)}, bf16[256,2048]{1,0:T(8,128)(2,1)}, u32[]{:S(2)}) %copy-start) | copy-done | bytes 1048600
  1.9 0.0 copy-start.1
  1.9 0.9 %copy-done.1 = bf16[256,256]{1,0:T(8,128)(2,1)S(1)} copy-done((bf16[256,256]{1,0:T(8,128)(2,1)S(1)}, bf16[256,256]{1,0:T(8,128)(2,1)}, u32[]{:S(2)}) %copy-start.1) | copy-done | bytes 131096
  2.8 0.0 copy-start.2
  2.8 0.7 copy-done.2
  3.5 0.0 copy-start.4
  3.5 0.7 copy-done.4
  4.1 28.5 %spread.1 = (bf16[2048,2048]{1,0:T(8,128)(2,1)S(1)}, bf16[2048,256]{1,0:T(8,128)(2,1)S(1)}, bf16[256,1024]{1,0:T(8,128)(2,1)S(1)}, f32[4,1,2048]{2,1,0:T(1,128)S(1)}, f32[8,2048]{1,0:T(8,128)S(1)}) custom-call(bf16[256,256]{1,0:T(8,128)(2,1)S(1)} %copy-done.1, bf16[8,256]{1,0:T(8,128)(2,1)S(1)} %copy-done.4, f32[1,2048]{1,0:T(1,128)S(1)} %bitcast.3, ...), custom_call_target="tpu_custom_call" | custom-call | flops 2147483648 | bytes 8388608 | tf_op jit(solution)/shard_map/spread/pallas_call | solution.py:480
  32.6 0.0 copy-start.3
  32.6 0.7 copy-done.3
  33.3 44.5 %assemble.1 = (f32[2,1024,1024]{2,1,0:T(8,128)}, f32[8,2048]{1,0:T(8,128)}, f32[2048,1024]{1,0:T(8,128)}) custom-call(bf16[2048,2048]{1,0:T(8,128)(2,1)S(1)} %get-tuple-element.11.phi, f32[8,2048]{1,0:T(8,128)S(1)} %get-tuple-element.12.sums, f32[1,2048]{1,0:T(1,128)S(1)} %bitcast.4, bf16[2048,256]{1,0:T(8,128)(2,1)S(1)} %get-tuple-element.13.points, ...), custom_call_target="tpu_custom_call" | custom-call | flops 128849018880 | bytes 33554432 | tf_op jit(solution)/shard_map/assemble/pallas_call | solution.py:618
Async XLA Ops:
  0.6 1.2 %copy-start = (bf16[256,2048]{1,0:T(8,128)(2,1)S(1)}, bf16[256,2048]{1,0:T(8,128)(2,1)}, u32[]{:S(2)}) copy-start(bf16[256,2048]{1,0:T(8,128)(2,1)} %freqs.1) | copy-start | bytes 3145732
  1.9 0.9 %copy-start.1 = (bf16[256,256]{1,0:T(8,128)(2,1)S(1)}, bf16[256,256]{1,0:T(8,128)(2,1)}, u32[]{:S(2)}) copy-start(bf16[256,256]{1,0:T(8,128)(2,1)} %points.1) | copy-start | bytes 393220
  2.8 0.7 copy-start.2
  3.5 0.7 copy-start.4
  32.6 0.7 copy-start.3

commit v3 on v2

--- a/solution.py
+++ b/solution.py
@@ -543,14 +543,10 @@
             phases[holder, :, pl.ds(pl.multiple_of(offset + j * WIDE, WIDE), WIDE)], scale
         )
 
-    def first(r, carry):
-        make(0, r)
-        return carry
-
-    lax.fori_loop(0, down, first, 0)
     for blk in range(count):
         base = blk * size
         for c in range(0, size, WIDE):
+            make(0, (base + c) // WIDE)
             mid = c + WIDE
             tile = across(phi[base : base + mid, :], phi[base + c : base + mid, :])
             work[blk, :mid, c:mid] = with_ridge(tile, ridge[:, base + c : base + mid], 0, c)

time: 78.3 us -> 76.8 us (0.981)
  Pallas kernels: 73 us -> 71.5 us
    pallas_call x1, Pallas kernels: 44.5 us -> 43 us  [assemble(): pl.pallas_call(functools.partial(assemble_body, count=count, size=size, s...]
where the time goes in v3:
time: 76.8 us; the launch traced here: 76.5 us
  Pallas kernels  71.5 us (93%)
  local copies, waits for them, and re-layouts  4.2 us (5%)
  between operations  0.82 us (1%)
    pallas_call x1, Pallas kernels, assemble(): pl.pallas_call(functools.partial(assemble_body, count=count, size=size, s...  43 us
    pallas_call x1, Pallas kernels, spread(): pl.pallas_call(functools.partial(spread_body, data_count=data_count, feat...  28.5 us
    unnamed x10, local copies, waits for them, and re-layouts  4.2 us

profile of v3, /device:TPU:18, one launch (start us, length us, event | category | flops | bytes accessed | tf_op | source)
XLA Modules:
  0.0 76.5 jit_solution(11979164902656294789)
XLA Ops:
  0.6 0.0 copy-start
  0.6 1.2 %copy-done = bf16[256,2048]{1,0:T(8,128)(2,1)S(1)} copy-done((bf16[256,2048]{1,0:T(8,128)(2,1)S(1)}, bf16[256,2048]{1,0:T(8,128)(2,1)}, u32[]{:S(2)}) %copy-start) | copy-done | bytes 1048600
  1.9 0.0 copy-start.1
  1.9 0.9 %copy-done.1 = bf16[256,256]{1,0:T(8,128)(2,1)S(1)} copy-done((bf16[256,256]{1,0:T(8,128)(2,1)S(1)}, bf16[256,256]{1,0:T(8,128)(2,1)}, u32[]{:S(2)}) %copy-start.1) | copy-done | bytes 131096
  2.8 0.0 copy-start.2
  2.8 0.7 copy-done.2
  3.5 0.0 copy-start.4
  3.5 0.7 copy-done.4
  4.1 28.5 %spread.1 = (bf16[2048,2048]{1,0:T(8,128)(2,1)S(1)}, bf16[2048,256]{1,0:T(8,128)(2,1)S(1)}, bf16[256,1024]{1,0:T(8,128)(2,1)S(1)}, f32[4,1,2048]{2,1,0:T(1,128)S(1)}, f32[8,2048]{1,0:T(8,128)S(1)}) custom-call(bf16[256,256]{1,0:T(8,128)(2,1)S(1)} %copy-done.1, bf16[8,256]{1,0:T(8,128)(2,1)S(1)} %copy-done.4, f32[1,2048]{1,0:T(1,128)S(1)} %bitcast.3, ...), custom_call_target="tpu_custom_call" | custom-call | flops 2147483648 | bytes 8388608 | tf_op jit(solution)/shard_map/spread/pallas_call | solution.py:480
  32.6 0.0 copy-start.3
  32.6 0.7 copy-done.3
  33.3 43.0 %assemble.1 = (f32[2,1024,1024]{2,1,0:T(8,128)}, f32[8,2048]{1,0:T(8,128)}, f32[2048,1024]{1,0:T(8,128)}) custom-call(bf16[2048,2048]{1,0:T(8,128)(2,1)S(1)} %get-tuple-element.11.phi, f32[8,2048]{1,0:T(8,128)S(1)} %get-tuple-element.12.sums, f32[1,2048]{1,0:T(1,128)S(1)} %bitcast.4, bf16[2048,256]{1,0:T(8,128)(2,1)S(1)} %get-tuple-element.13.points, ...), custom_call_target="tpu_custom_call" | custom-call | flops 128849018880 | bytes 33554432 | tf_op jit(solution)/shard_map/assemble/pallas_call | solution.py:614
Async XLA Ops:
  0.6 1.2 %copy-start = (bf16[256,2048]{1,0:T(8,128)(2,1)S(1)}, bf16[256,2048]{1,0:T(8,128)(2,1)}, u32[]{:S(2)}) copy-start(bf16[256,2048]{1,0:T(8,128)(2,1)} %freqs.1) | copy-start | bytes 3145732
  1.9 0.9 %copy-start.1 = (bf16[256,256]{1,0:T(8,128)(2,1)S(1)}, bf16[256,256]{1,0:T(8,128)(2,1)}, u32[]{:S(2)}) copy-start(bf16[256,256]{1,0:T(8,128)(2,1)} %points.1) | copy-start | bytes 393220
  2.8 0.7 copy-start.2
  3.5 0.7 copy-start.4
  32.6 0.7 copy-start.3

commit v4 on v3

--- a/solution.py
+++ b/solution.py
@@ -287,7 +287,7 @@
 
 
 def spread_body(points, targets, phase, freqs, phi, points_out, freqs_out, turns_out, projected,
-                pbuf, tbuf, fbuf, fown, cbuf, flipped, turns, in_sem,
+                pbuf, tbuf, fbuf, cbuf, flipped, turns, in_sem,
                 psend, precv, tsend, trecv, fsend, frecv, csend, crecv, pass_sem,
                 *, data_count, feat_count, scale):
     me = lax.axis_index("dp")
@@ -310,7 +310,6 @@
         pltpu.make_async_copy(points, pbuf.at[me], in_sem.at[0]),
         pltpu.make_async_copy(targets, tbuf.at[me], in_sem.at[1]),
         pltpu.make_async_copy(phase, fbuf.at[here], in_sem.at[2]),
-        pltpu.make_async_copy(freqs, fown, in_sem.at[3]),
     ]
     for copy in loads:
         copy.start()
@@ -346,7 +345,7 @@
         return remote(fbuf.at[slot], fbuf.at[slot], fsend.at[step], frecv.at[slot], me, feat)
 
     def freqs_copy(q, way, feat):
-        source = fown.at[:, pl.ds(offset + q * piece, piece)]
+        source = freqs.at[:, pl.ds(offset + q * piece, piece)]
         return remote(source, cbuf.at[q], csend.at[way * pieces + q], crecv.at[q], me, feat)
 
     def freqs_pass(q, t):
@@ -363,7 +362,6 @@
     loads[2].wait()
     for step in range(1, feat_count):
         phase_copy(here, step).start()
-    loads[3].wait()
     near_x = (1 - holder % 2) + holder // 2 * 2
     near_y = holder % 2 + (1 - holder // 2) * 2
     sends = [(q, 0, near_x) for q in range(pieces)]
@@ -375,7 +373,7 @@
         for q, way, feat in sends:
             freqs_copy(q, way, feat).start()
 
-    flipped[...] = fown[...].T
+    flipped[...] = freqs[...].T
     for first in range(0, width, TILE):
         row = fbuf[here, :, first : first + TILE] * (0.5 / math.pi)
         turns[first : first + TILE, :] = jnp.broadcast_to(row, (TILE, TILE)).T
@@ -437,7 +435,7 @@
 
     @pl.when(here == holder)
     def _():
-        freqs_out[...] = fown[:, pl.ds(offset, tile_width)]
+        freqs_out[...] = freqs[:, pl.ds(offset, tile_width)]
         for q, way, feat in sends:
             freqs_copy(q, way, feat).wait_send()
 
@@ -486,17 +484,16 @@
             jax.ShapeDtypeStruct((feat_count, 1, width), jnp.float32),
             jax.ShapeDtypeStruct((outs, width), jnp.float32),
         ),
-        in_specs=[hbm] * 4,
+        in_specs=[hbm] * 3 + [vmem],
         out_specs=[vmem] * 5,
         scratch_shapes=[
             pltpu.VMEM((data_count, rows, depth), jnp.bfloat16),
             pltpu.VMEM((data_count, outs, rows), jnp.bfloat16),
             pltpu.VMEM((feat_count, 1, width), jnp.float32),
-            pltpu.VMEM((depth, width), jnp.bfloat16),
             pltpu.VMEM((pieces, depth, tile_width // pieces), jnp.bfloat16),
             pltpu.VMEM((width, depth), jnp.bfloat16),
             pltpu.VMEM((width, TILE), jnp.float32),
-            dma((4,)),
+            dma((3,)),
             dma((data_count // 2,)),
             dma((data_count,)),
             dma((data_count,)),

time: 76.8 us -> 76.8 us (level)
  no operation moved by 1% of the time
where the time goes in v4:
time: 76.8 us; the launch traced here: 76.5 us
  Pallas kernels  71.4 us (93%)
  local copies, waits for them, and re-layouts  4.2 us (5%)
  between operations  0.82 us (1%)
    pallas_call x1, Pallas kernels, assemble(): pl.pallas_call(functools.partial(assemble_body, count=count, size=size, s...  43.1 us
    pallas_call x1, Pallas kernels, spread(): pl.pallas_call(functools.partial(spread_body, data_count=data_count, feat...  28.4 us
    unnamed x10, local copies, waits for them, and re-layouts  4.2 us

profile of v4, /device:TPU:18, one launch (start us, length us, event | category | flops | bytes accessed | tf_op | source)
XLA Modules:
  0.0 76.5 jit_solution(8271286585386268130)
XLA Ops:
  0.6 0.0 copy-start
  0.6 1.2 %copy-done = bf16[256,2048]{1,0:T(8,128)(2,1)S(1)} copy-done((bf16[256,2048]{1,0:T(8,128)(2,1)S(1)}, bf16[256,2048]{1,0:T(8,128)(2,1)}, u32[]{:S(2)}) %copy-start) | copy-done | bytes 1048600
  1.9 0.0 copy-start.1
  1.9 0.9 %copy-done.1 = bf16[256,256]{1,0:T(8,128)(2,1)S(1)} copy-done((bf16[256,256]{1,0:T(8,128)(2,1)S(1)}, bf16[256,256]{1,0:T(8,128)(2,1)}, u32[]{:S(2)}) %copy-start.1) | copy-done | bytes 131096
  2.8 0.0 copy-start.2
  2.8 0.7 copy-done.2
  3.5 0.0 copy-start.4
  3.5 0.7 copy-done.4
  4.1 28.4 %spread.1 = (bf16[2048,2048]{1,0:T(8,128)(2,1)S(1)}, bf16[2048,256]{1,0:T(8,128)(2,1)S(1)}, bf16[256,1024]{1,0:T(8,128)(2,1)S(1)}, f32[4,1,2048]{2,1,0:T(1,128)S(1)}, f32[8,2048]{1,0:T(8,128)S(1)}) custom-call(bf16[256,256]{1,0:T(8,128)(2,1)S(1)} %copy-done.1, bf16[8,256]{1,0:T(8,128)(2,1)S(1)} %copy-done.4, f32[1,2048]{1,0:T(1,128)S(1)} %bitcast.3, ...), custom_call_target="tpu_custom_call" | custom-call | flops 2147483648 | bytes 8388608 | tf_op jit(solution)/shard_map/spread/pallas_call | solution.py:478
  32.5 0.0 copy-start.3
  32.6 0.7 copy-done.3
  33.2 43.1 %assemble.1 = (f32[2,1024,1024]{2,1,0:T(8,128)}, f32[8,2048]{1,0:T(8,128)}, f32[2048,1024]{1,0:T(8,128)}) custom-call(bf16[2048,2048]{1,0:T(8,128)(2,1)S(1)} %get-tuple-element.11.phi, f32[8,2048]{1,0:T(8,128)S(1)} %get-tuple-element.12.sums, f32[1,2048]{1,0:T(1,128)S(1)} %bitcast.4, bf16[2048,256]{1,0:T(8,128)(2,1)S(1)} %get-tuple-element.13.points, ...), custom_call_target="tpu_custom_call" | custom-call | flops 128849018880 | bytes 33554432 | tf_op jit(solution)/shard_map/assemble/pallas_call | solution.py:611
Async XLA Ops:
  0.6 1.2 %copy-start = (bf16[256,2048]{1,0:T(8,128)(2,1)S(1)}, bf16[256,2048]{1,0:T(8,128)(2,1)}, u32[]{:S(2)}) copy-start(bf16[256,2048]{1,0:T(8,128)(2,1)} %freqs.1) | copy-start | bytes 3145732
  1.9 0.9 %copy-start.1 = (bf16[256,256]{1,0:T(8,128)(2,1)S(1)}, bf16[256,256]{1,0:T(8,128)(2,1)}, u32[]{:S(2)}) copy-start(bf16[256,256]{1,0:T(8,128)(2,1)} %points.1) | copy-start | bytes 393220
  2.8 0.7 copy-start.2
  3.5 0.7 copy-start.4
  32.5 0.7 copy-start.3
